TPU v7x, 32 devices: a whole 2x2x4 slice. The times are simulated.
32 devices in a mesh: ga: 2 (over core), band: 16 (over z, y, x).
Axes of the slice: x: 2, y: 2, z: 4, core: 2. Of those that a mesh axis runs over, the one named last changes fastest.
Arguments:
- orbitals: bfloat16 [1024, 2, 16384], P('band', None, 'ga'), may hold values from -6 to 6
- projectors: bfloat16 [864, 2, 16384], P(None, None, ('ga', 'band')), may hold values from -0.03125 to 0.03125
- coupling: float32 [4, 18, 18], replicated, may hold values from -6 to 6
- species: int32 [48], replicated, may hold values from 0 to 3
- offsets: int32 [48], replicated, may hold values from 0 to 846, as said below
Outputs:
- applied: bfloat16 [1024, 2, 16384], P('band', None, 'ga')
Inputs may be any that keep to these rules, and one draw needn't show every extreme that they name: Each atom's 18 projectors are the 18 consecutive rows of projectors starting at its offset; offsets are multiples of 18, and the atoms' blocks are distinct and cover all 864 rows.
All inputs are finite; a program needn't handle non-finite values.
Results may differ from a plain program's by a relative error of at most 0.0049.
Values may be sent and summed in bfloat16 or wider, within the bound.
A program may use at most 64 MiB of HBM per device.

v0:
```python
import jax
import jax.numpy as jnp
from jax import lax
from jax.sharding import PartitionSpec as P


def block_matrices(coupling, species, offsets):
    per_atom = coupling.shape[1]
    count = offsets.shape[0]
    blocks = jnp.arange(count, dtype=jnp.int32)
    matches = (offsets[None, :] == blocks[:, None] * per_atom).astype(jnp.int32)
    atom_kind = jnp.sum(matches * species[None, :], axis=1)
    onehot = (atom_kind[:, None] == jnp.arange(coupling.shape[0], dtype=jnp.int32)[None, :]).astype(
        jnp.float32
    )
    table = coupling.reshape(coupling.shape[0], per_atom * per_atom)
    picked = jnp.dot(
        onehot, table, precision=lax.Precision.HIGHEST, preferred_element_type=jnp.float32
    )
    return picked.reshape(count, per_atom, per_atom)


def apply_coupling(matrices, becp):
    count = matrices.shape[0]
    per_atom = matrices.shape[1]
    height = becp.shape[0]
    widths = becp.shape[2]
    blocked = becp.reshape(count, per_atom, 2 * widths)
    coupled = jnp.einsum("aij,ajc->aic", matrices, blocked, precision=lax.Precision.HIGHEST)
    return coupled.reshape(height, 2, widths).astype(jnp.bfloat16)


def project_bands(projectors, spread):
    total_proj = projectors.shape[0]
    total_bands = spread.shape[0]
    flat_proj = projectors.reshape(total_proj, -1)
    turned = jnp.concatenate([spread[:, 1, :], -spread[:, 0, :]], axis=1)
    stacked = jnp.concatenate([spread.reshape(total_bands, -1), turned], axis=0)
    partial_value = lax.dot_general(
        flat_proj, stacked, (((1,), (1,)), ((), ())), preferred_element_type=jnp.float32
    )
    return partial_value.reshape(total_proj, 2, total_bands)


def add_back(projectors, dbecp):
    total_proj = projectors.shape[0]
    total_bands = dbecp.shape[2]
    columns = dbecp.reshape(total_proj, 2 * total_bands)
    real_part = lax.dot_general(
        columns, projectors[:, 0, :], (((0,), (0,)), ((), ())), preferred_element_type=jnp.float32
    )
    imag_part = lax.dot_general(
        columns, projectors[:, 1, :], (((0,), (0,)), ((), ())), preferred_element_type=jnp.float32
    )
    out_real = real_part[:total_bands] - imag_part[total_bands:]
    out_imag = imag_part[:total_bands] + real_part[total_bands:]
    return jnp.stack([out_real, out_imag], axis=1).astype(jnp.bfloat16)


def per_device(orbitals, projectors, coupling, species, offsets):
    matrices = block_matrices(coupling, species, offsets)
    spread = lax.all_to_all(orbitals, "band", split_axis=2, concat_axis=0, tiled=True)
    partial_value = project_bands(projectors, spread)
    becp = lax.psum(partial_value, ("ga", "band"))
    dbecp = apply_coupling(matrices, becp)
    result = add_back(projectors, dbecp)
    return lax.all_to_all(result, "band", split_axis=0, concat_axis=2, tiled=True)


def solution(mesh):
    placed = (P("band", None, "ga"), P(None, None, ("ga", "band")), P(), P(), P())
    return jax.shard_map(
        per_device, mesh=mesh, in_specs=placed, out_specs=P("band", None, "ga"), check_vma=False
    )
```

profile of v0, /device:TPU:0, one launch (start us, length us, event | category | flops | bytes accessed | tf_op | source)
XLA Modules:
  0.0 417.0 jit_solution(8911082358564989493)
XLA Ops:
  6.5 11.4 %copy.45 = bf16[64,2,8192]{0,1,2:T(2,128)(2,1)} copy(bf16[64,2,8192]{2,1,0:T(2,128)(2,1)} %param.5) | data formatting | bytes 4194304 | tf_op args[0]
  17.9 7.5 %reshape.39 = bf16[16,2,32768]{2,1,0:T(2,128)(2,1)} reshape(bf16[8192,2,64]{2,1,0:T(2,128)(2,1)} %bitcast.46) | data formatting | bytes 4194304
  25.4 0.0 copy-start
  25.4 8.5 %all-to-all-start = ((bf16[16,2,32768]{2,1,0:T(2,128)(2,1)}), bf16[16,2,32768]{2,1,0:T(2,128)(2,1)}, u32[]{:S(2)}, u32[]{:S(2)}) async-start(bf16[16,2,32768]{2,1,0:T(2,128)(2,1)} %reshape.39), calls=%async_computation | async-start | bytes 4194304 | tf_op jit(solution)/shard_map/all_to_all | solution.py:62
  34.0 0.0 all-reduce.2.cloned.1.call-start
  34.0 0.0 copy-done
  34.0 0.5 copy.60
  34.5 42.6 %all-to-all-done = bf16[16,2,32768]{2,1,0:T(2,128)(2,1)} async-done(((bf16[16,2,32768]{2,1,0:T(2,128)(2,1)}), bf16[16,2,32768]{2,1,0:T(2,128)(2,1)}, u32[]{:S(2)}, u32[]{:S(2)}) %all-to-all-start) | async-done | bytes 2097184 | tf_op jit(solution)/shard_map/all_to_all | solution.py:62
  77.1 7.4 %reshape.40 = bf16[8192,2,64]{2,1,0:T(2,128)(2,1)} reshape(bf16[16,2,32768]{2,1,0:T(2,128)(2,1)} %all-to-all-done) | data formatting | bytes 4194304
  84.4 10.6 %copy.55 = bf16[64,2,16,512]{3,0,2,1:T(8,128)(2,1)} copy(bf16[64,2,16,512]{0,1,3,2:T(2,128)(2,1)} %bitcast.44) | data formatting | bytes 4194304 | tf_op jit(solution)/shard_map/all_to_all | solution.py:62
  95.0 7.4 %copy.54 = bf16[64,2,16,512]{3,2,0,1:T(8,128)(2,1)} copy(bf16[64,2,16,512]{0,1,3,2:T(2,128)(2,1)} %bitcast.45) | data formatting | bytes 4194304 | tf_op jit(solution)/shard_map/all_to_all | solution.py:62
  102.4 0.0 copy-start.1
  102.4 1.8 slice_bitcast_fusion
  104.2 0.4 copy-done.1
  104.6 2.2 copy.47
  106.8 0.6 copy.59
  107.4 12.5 %fusion.6 = f32[864,2048]{1,0:T(8,128)} fusion(bf16[864,1024]{1,0:T(8,128)(2,1)S(1)} %bitcast.53, bf16[1024,512]{1,0:T(8,128)(2,1)S(1)} %get-tuple-element.8, bf16[1024,512]{1,0:T(8,128)(2,1)S(1)} %get-tuple-element.7, bf16[1024,1024]{1,0:T(8,128)(2,1)S(1)} %bitcast.52), kind=kOutput, calls=%fused_computation.6 | convolution fusion | flops 3636461568 | bytes 13041664 | tf_op jit(solution)/shard_map/dot_general | solution.py:39
  119.9 7.9 %reshape.36 = f32[48,18,2048]{2,1,0:T(8,128)} reshape(f32[864,2048]{1,0:T(8,128)} %fusion.6) | data formatting | bytes 14155776 | tf_op jit(solution)/shard_map/reshape | solution.py:28
  127.8 0.0 copy-start.5
  127.8 0.0 copy-start.6
  127.8 0.0 copy-start.7
  127.8 0.0 all-reduce.2.cloned.1.call-update
  127.8 0.7 copy-done.5
  128.6 0.1 reshape.32
  128.6 0.1 dot_general.22
  128.8 0.0 copy-done.6
  128.8 0.0 copy-done.7
  128.8 0.2 select_reduce_fusion
  128.9 0.4 fusion.16
  129.4 0.3 copy.49
  129.7 4.2 %fusion.22 = (bf16[864,1,512]{2,1,0:T(2,128)(2,1)}, bf16[864,1,512]{2,1,0:T(2,128)(2,1)}) fusion(bf16[864,2,512]{2,1,0:T(2,128)(2,1)S(1)} %copy-done), kind=kLoop, calls=%fused_computation.30 | loop fusion | bytes 3538944 | tf_op jit(solution)/shard_map/slice | solution.py:53
  133.9 189.5 %all-reduce.2.cloned.1.call-done = f32[48,18,2048]{2,1,0:T(8,128)} async-done(((f32[48,18,2048]{2,1,0:T(8,128)}), f32[48,18,2048]{2,1,0:T(8,128)}) %all-reduce.2.cloned.1.call-update) | async-done | bytes 7077904 | tf_op jit(solution)/shard_map/psum | solution.py:64
  323.4 12.2 %convolution_convert_fusion = bf16[48,18,2048]{2,1,0:T(8,128)(2,1)} fusion(f32[48,18,18]{2,1,0:T(8,128)S(1)} %copy.49, f32[48,18,2048]{2,1,0:T(8,128)} %all-reduce.2.cloned.1.call-done), kind=kOutput, calls=%fused_computation.7 | convolution fusion | flops 383975424 | bytes 10679040 | tf_op jit(solution)/shard_map/aij,ajc->aic/dot_general | solution.py:29
  335.5 0.0 copy-start.4
  335.5 6.2 %convert_element_type.12 = bf16[864,2048]{1,0:T(8,128)(2,1)} reshape(bf16[48,18,2048]{2,1,0:T(8,128)(2,1)} %convolution_convert_fusion) | data formatting | bytes 7077888 | tf_op jit(solution)/shard_map/convert_element_type | solution.py:30
  341.7 0.0 copy-done.4
  341.7 0.0 copy-start.2
  341.7 0.0 copy-start.3
  341.8 4.6 %fusion.14 = f32[2048,512]{1,0:T(8,128)S(1)} fusion(bf16[864,2048]{1,0:T(8,128)(2,1)} %convert_element_type.12, bf16[864,1,512]{2,1,0:T(2,128)(2,1)S(1)} %copy-done.4), kind=kOutput, calls=%fused_computation.19 | convolution fusion | flops 1811939328 | bytes 8617984 | tf_op jit(solution)/shard_map/dot_general | solution.py:52
  346.3 0.0 copy-done.2
  346.4 0.0 copy-done.3
  346.4 2.4 fusion.15
  348.8 1.2 fusion.11
  350.0 0.2 pad_maximum_fusion
  350.2 2.2 copy.52
  352.4 54.2 %all_to_all.36 = bf16[1024,2,512]{2,1,0:T(2,128)(2,1)S(1)} all-to-all(bf16[1024,2,512]{2,1,0:T(2,128)(2,1)S(1)} %copy.52), channel_id=1, replica_groups=mesh['ga'=2,'band'=16] {'band'}, dimensions={0} | all-to-all | bytes 4194304 | tf_op jit(solution)/shard_map/all_to_all | solution.py:67
  406.5 3.6 copy.58
  (2 shorter events, 0.0 us)
Async XLA Ops:
  25.4 8.6 %copy-start = (bf16[864,2,512]{2,1,0:T(2,128)(2,1)S(1)}, bf16[864,2,512]{2,1,0:T(2,128)(2,1)}, u32[]{:S(2)}) copy-start(bf16[864,2,512]{2,1,0:T(2,128)(2,1)} %param.6) | copy-start | bytes 5308420
  25.4 51.6 %all-to-all-start = ((bf16[16,2,32768]{2,1,0:T(2,128)(2,1)}), bf16[16,2,32768]{2,1,0:T(2,128)(2,1)}, u32[]{:S(2)}, u32[]{:S(2)}) async-start(bf16[16,2,32768]{2,1,0:T(2,128)(2,1)} %reshape.39), calls=%async_computation | async-start | bytes 4194304 | tf_op jit(solution)/shard_map/all_to_all | solution.py:62
  34.0 289.4 %all-reduce.2.cloned.1.call-start = ((), (), s32[]{:S(2)}) async-start(), calls=%async_computation.2 | async-start | bytes 18874368 | tf_op jit(solution)/shard_map/psum | solution.py:64
  102.4 2.2 copy-start.1
  127.8 0.8 copy-start.5
  127.8 1.0 copy-start.6
  127.8 1.0 copy-start.7
  335.5 6.2 %copy-start.4 = (bf16[864,1,512]{2,1,0:T(2,128)(2,1)S(1)}, bf16[864,1,512]{2,1,0:T(2,128)(2,1)}, u32[]{:S(2)}) copy-start(bf16[864,1,512]{2,1,0:T(2,128)(2,1)} %get-tuple-element.9) | copy-start | bytes 2654212
  341.7 4.6 %copy-start.2 = (bf16[864,2048]{1,0:T(8,128)(2,1)S(1)}, bf16[864,2048]{1,0:T(8,128)(2,1)}, u32[]{:S(2)}) copy-start(bf16[864,2048]{1,0:T(8,128)(2,1)} %convert_element_type.12) | copy-start | bytes 10616836
  341.7 4.6 %copy-start.3 = (bf16[864,1,512]{2,1,0:T(2,128)(2,1)S(1)}, bf16[864,1,512]{2,1,0:T(2,128)(2,1)}, u32[]{:S(2)}) copy-start(bf16[864,1,512]{2,1,0:T(2,128)(2,1)} %get-tuple-element.10) | copy-start | bytes 2654212
Sparse Core Ops, SparseCore 0:
  127.9 195.3 all-reduce.1
where the time goes:
time: 419 us; the launch traced here: 417 us
  waiting for transfers between devices  232 us (55%)
  local copies, waits for them, and re-layouts  73.2 us (17%)
  blocking collectives  54.2 us (13%)
  matrix products  32 us (8%)
  between operations  13.6 us (3%)
  starting transfers between devices  8.57 us (2%)
    psum x1, waiting for transfers between devices, per_device(): becp = lax.psum(partial_value, ('ga', 'band'))  189 us
    all_to_all x1, blocking collectives, per_device(): lax.all_to_all(result, 'band', split_axis=0, concat_axis=2, tiled=True)  54.2 us
    all_to_all x1, waiting for transfers between devices, per_device(): lax.all_to_all(orbitals, 'band', split_axis=2, concat_axis=0, tiled=True)  42.6 us
    unnamed x22, local copies, waits for them, and re-layouts  28.5 us
    all_to_all x3, local copies, waits for them, and re-layouts, per_device(): lax.all_to_all(orbitals, 'band', split_axis=2, concat_axis=0, tiled=True)  20.1 us
    dot_general x1, matrix products, project_bands(): lax.dot_general(flat_proj, stacked, (((1,), (1,)), ((), ())), preferred_e...  12.5 us
    dot_general x1, matrix products, apply_coupling(): jnp.einsum('aij,ajc->aic', matrices, blocked, precision=lax.Precision.HIG...  12.2 us
    all_to_all x1, starting transfers between devices, per_device(): lax.all_to_all(orbitals, 'band', split_axis=2, concat_axis=0, tiled=True)  8.52 us
  transfers between devices with their start and end apart: 2, of which 2 were waited for; matrix products, arithmetic and copies ran while one was open for 1% of the time, Pallas kernels for 0%

commit v1 on v0

--- a/solution.py
+++ b/solution.py
@@ -2,6 +2,19 @@
 import jax.numpy as jnp
 from jax import lax
 from jax.sharding import PartitionSpec as P
+
+
+def scenes_advance(local, k_dim, page):
+    y1, z1 = (local.shape[:k_dim], local.shape[k_dim + 1 :])
+    met_up = jnp.moveaxis(local.reshape(*y1, page, -1, *z1), k_dim, 0)
+    return met_up
+
+
+def _choose_chunk(v0, d_out):
+    y2 = list(v0.shape[1:])
+    y2[d_out] *= v0.shape[0]
+    big = jnp.moveaxis(v0, 0, d_out).reshape(y2)
+    return big
 
 
 def block_matrices(coupling, species, offsets):
@@ -58,8 +71,20 @@
 
 
 def per_device(orbitals, projectors, coupling, species, offsets):
+
+    def serve_sources_all(vals, ax_name, row_data, load):
+        heard, lower = (lax.axis_size(ax_name), lax.axis_index(ax_name))
+        fresh = scenes_advance(vals, row_data, heard)
+        stack_in = [fresh[lower]]
+        for b in range(1, heard):
+            u_next = fresh[lower ^ b]
+            stack_in.append(lax.ppermute(u_next, ax_name, [(d, d ^ b) for d in range(heard)]))
+        fresh = jnp.stack(stack_in)[lower ^ jnp.arange(heard)]
+        block_next = _choose_chunk(fresh, load)
+        return block_next
+
     matrices = block_matrices(coupling, species, offsets)
-    spread = lax.all_to_all(orbitals, "band", split_axis=2, concat_axis=0, tiled=True)
+    spread = serve_sources_all(orbitals, "band", 2, 0)
     partial_value = project_bands(projectors, spread)
     becp = lax.psum(partial_value, ("ga", "band"))
     dbecp = apply_coupling(matrices, becp)

time: 419 us -> 389 us (0.928)
  waiting for transfers between devices: 232 us -> 202 us
  starting transfers between devices: 8.57 us -> 33 us
  local copies, waits for them, and re-layouts: 73.2 us -> 52.5 us
    all_to_all x1 -> x0, waiting for transfers between devices: 42.6 us -> none  [per_device(): lax.all_to_all(orbitals, 'band', split_axis=2, concat_axis=0, tiled=True)]
    ppermute x0 -> x15, starting transfers between devices: none -> 33 us  [serve_sources_all(): lax.ppermute(u_next, ax_name, [(d, d ^ b) for d in range(heard)])]
    all_to_all x3 -> x0, local copies, waits for them, and re-layouts: 20.1 us -> none  [per_device(): lax.all_to_all(orbitals, 'band', split_axis=2, concat_axis=0, tiled=True)]
    ppermute x0 -> x15, waiting for transfers between devices: none -> 13.7 us  [serve_sources_all(): lax.ppermute(u_next, ax_name, [(d, d ^ b) for d in range(heard)])]
    unnamed x22 -> x47, local copies, waits for them, and re-layouts: 28.5 us -> 14.9 us
    all_to_all x1 -> x0, starting transfers between devices: 8.52 us -> none  [per_device(): lax.all_to_all(orbitals, 'band', split_axis=2, concat_axis=0, tiled=True)]
    another operation x0 -> x2, local copies, waits for them, and re-layouts: none -> 6.82 us
    gather x0 -> x3, local copies, waits for them, and re-layouts: none -> 4.66 us  [serve_sources_all(): fresh = jnp.stack(stack_in)[lower ^ jnp.arange(heard)]]
  transfers between devices with their start and end apart: 2 -> 16, of which waited for: 2 -> 4; matrix products, arithmetic and copies ran while one was open for 1% -> 5% of each run, Pallas kernels for 0% -> 0%
where the time goes in v1:
time: 389 us
  waiting for transfers between devices  202 us (52%)
  blocking collectives  54.2 us (14%)
  local copies, waits for them, and re-layouts  52.5 us (13%)
  starting transfers between devices  33 us (8%)
  matrix products  31.4 us (8%)
  between operations  13.8 us (4%)
    psum x1, waiting for transfers between devices, per_device(): becp = lax.psum(partial_value, ('ga', 'band'))  188 us
    all_to_all x1, blocking collectives, per_device(): lax.all_to_all(result, 'band', split_axis=0, concat_axis=2, tiled=True)  54.2 us
    ppermute x15, starting transfers between devices, serve_sources_all(): lax.ppermute(u_next, ax_name, [(d, d ^ b) for d in range(heard)])  33 us
    unnamed x47, local copies, waits for them, and re-layouts  14.9 us
    ppermute x15, waiting for transfers between devices, serve_sources_all(): lax.ppermute(u_next, ax_name, [(d, d ^ b) for d in range(heard)])  13.7 us
    dot_general x1, matrix products, project_bands(): lax.dot_general(flat_proj, stacked, (((1,), (1,)), ((), ())), preferred_e...  12.4 us
    dot_general x1, matrix products, apply_coupling(): jnp.einsum('aij,ajc->aic', matrices, blocked, precision=lax.Precision.HIG...  12.1 us
    reshape x1, local copies, waits for them, and re-layouts, apply_coupling(): blocked = becp.reshape(count, per_atom, 2 * widths)  7.9 us
  transfers between devices with their start and end apart: 16, of which 4 were waited for; matrix products, arithmetic and copies ran while one was open for 5% of the time, Pallas kernels for 0%

profile of v1, /device:TPU:0, one launch (start us, length us, event | category | flops | bytes accessed | tf_op | source)
XLA Modules:
  0.0 388.5 jit_solution(12306712407268415423)
XLA Ops:
  6.5 3.2 reshape.97
  9.9 6.2 %constant_dynamic-slice_fusion = (bf16[64,2,1,512]{3,2,1,0:T(2,128)(2,1)S(1)}, bf16[64,2,1,512]{3,2,1,0:T(2,128)(2,1)S(1)}, bf16[64,2,1,512]{3,2,1,0:T(2,128)(2,...) fusion(bf16[64,2,16,512]{3,2,1,0:T(8,128)(2,1)S(1)} %reshape.97, ...), kind=kLoop, calls=%fused_computation.59 | loop fusion | bytes 4194368 | tf_op jit(solution)/shard_map/dynamic-slice.15
  16.1 3.0 collective-permute-start
  19.1 1.6 collective-permute-start.1
  20.8 0.1 collective-permute-start.2
  20.9 2.1 collective-permute-start.3
  23.0 1.4 collective-permute-start.4
  24.5 0.7 fusion.16
  25.7 0.3 copy-done
  26.0 1.7 copy.126
  27.7 0.0 collective-permute-done
  27.7 2.6 collective-permute-start.5
  30.3 0.7 bitcast_dynamic-update-slice_fusion.14
  31.0 0.0 collective-permute-done.1
  31.0 0.7 bitcast_dynamic-update-slice_fusion.13
  31.7 3.0 collective-permute-start.7
  34.6 0.7 bitcast_dynamic-update-slice_fusion.12
  35.3 1.3 collective-permute-start.8
  36.6 0.7 bitcast_dynamic-update-slice_fusion.11
  37.2 3.5 collective-permute-start.9
  40.8 0.7 bitcast_dynamic-update-slice_fusion.10
  41.4 0.7 bitcast_dynamic-update-slice_fusion.9
  42.1 3.8 collective-permute-start.11
  46.0 0.7 bitcast_dynamic-update-slice_fusion.8
  46.6 7.1 %collective-permute-done.7 = bf16[64,2,512]{2,0,1:T(8,128)(2,1)S(1)} collective-permute-done((bf16[64,2,512]{2,0,1:T(8,128)(2,1)S(1)}, bf16[64,2,512]{2,0,1:T(8,128)(2,1)S(1)}, u32[]{:S(2)}, u32[]{:S(2)}) %collective-permute-start.7) | collective-permute-done | bytes 131104 | tf_op jit(solution)/shard_map/ppermute | solution.py:81
  53.7 3.9 %collective-permute-start.12 = (bf16[64,2,512]{2,0,1:T(8,128)(2,1)S(1)}, bf16[64,2,512]{2,0,1:T(8,128)(2,1)S(1)}, u32[]{:S(2)}, u32[]{:S(2)}) collective-permute-start(bf16[64,2,512]{2,0,1:T(8,128)(2,1)S(1)} %bitcast.143), channel_id=1, source_target_pairs={{0,13},{1,12},{2,15},{3,14},{4,9},{5,8},{6,11},{7,10},{8,5},{9,4},... | collective-permute-start | bytes 393224 | tf_op jit(solution)/shard_map/ppermute | solution.py:81
  57.6 0.7 bitcast_dynamic-update-slice_fusion.7
  58.3 2.9 collective-permute-start.13
  61.2 0.7 bitcast_dynamic-update-slice_fusion.6
  61.8 5.0 %collective-permute-done.9 = bf16[64,2,512]{2,0,1:T(8,128)(2,1)S(1)} collective-permute-done((bf16[64,2,512]{2,0,1:T(8,128)(2,1)S(1)}, bf16[64,2,512]{2,0,1:T(8,128)(2,1)S(1)}, u32[]{:S(2)}, u32[]{:S(2)}) %collective-permute-start.9) | collective-permute-done | bytes 131104 | tf_op jit(solution)/shard_map/ppermute | solution.py:81
  66.8 3.7 collective-permute-start.14
  70.6 0.7 bitcast_dynamic-update-slice_fusion.5
  71.2 0.7 bitcast_dynamic-update-slice_fusion.4
  71.9 0.7 bitcast_dynamic-update-slice_fusion.3
  72.6 0.7 bitcast_dynamic-update-slice_fusion.2
  73.2 0.7 bitcast_dynamic-update-slice_fusion.1
  73.9 1.6 collective-permute-done.14
  75.5 0.7 bitcast_dynamic-update-slice_fusion
  76.2 2.3 gather_fusion
  78.5 0.2 copy.35
  78.7 2.2 copy.34
  80.9 0.1 slice_bitcast_fusion
  81.0 0.6 copy.125
  81.6 0.9 copy-done.3
  82.5 12.4 %fusion.6 = f32[864,2048]{1,0:T(8,128)} fusion(bf16[864,1024]{1,0:T(8,128)(2,1)S(1)} %bitcast.140, bf16[1024,512]{1,0:T(8,128)(2,1)S(1)} %get-tuple-element.8, bf16[1024,512]{1,0:T(8,128)(2,1)S(1)} %get-tuple-element.7, bf16[1024,1024]{1,0:T(8,128)(2,1)S(1)} %bitcast.139), kind=kOutput, calls=%fused_computation.7 | convolution fusion | flops 3636461568 | bytes 13041664 | tf_op jit(solution)/shard_map/dot_general | solution.py:52
  94.8 7.9 %reshape.86 = f32[48,18,2048]{2,1,0:T(8,128)} reshape(f32[864,2048]{1,0:T(8,128)} %fusion.6) | data formatting | bytes 14155776 | tf_op jit(solution)/shard_map/reshape | solution.py:41
  102.8 0.0 all-reduce.2.cloned.1.call-update
  102.8 0.7 copy-done.4
  103.5 0.1 reshape.81
  103.6 0.1 dot_general.22
  103.7 0.2 select_reduce_fusion
  103.9 0.4 fusion.17
  104.3 0.3 copy.36
  104.6 4.2 %fusion.24 = (bf16[864,1,512]{2,1,0:T(2,128)(2,1)}, bf16[864,1,512]{2,1,0:T(2,128)(2,1)}) fusion(bf16[864,2,512]{2,1,0:T(2,128)(2,1)S(1)} %copy-done.1), kind=kLoop, calls=%fused_computation.82 | loop fusion | bytes 3538944 | tf_op jit(solution)/shard_map/slice | solution.py:66
  108.9 188.2 %all-reduce.2.cloned.1.call-done = f32[48,18,2048]{2,1,0:T(8,128)} async-done(((f32[48,18,2048]{2,1,0:T(8,128)}), f32[48,18,2048]{2,1,0:T(8,128)}) %all-reduce.2.cloned.1.call-update) | async-done | bytes 7077904 | tf_op jit(solution)/shard_map/psum | solution.py:89
  297.1 12.1 %convolution_convert_fusion = bf16[48,18,2048]{2,1,0:T(8,128)(2,1)} fusion(f32[48,18,18]{2,1,0:T(8,128)S(1)} %copy.36, f32[48,18,2048]{2,1,0:T(8,128)} %all-reduce.2.cloned.1.call-done), kind=kOutput, calls=%fused_computation.8 | convolution fusion | flops 383975424 | bytes 10679040 | tf_op jit(solution)/shard_map/aij,ajc->aic/dot_general | solution.py:42
  309.2 4.5 %convert_element_type.12 = bf16[864,2048]{1,0:T(8,128)(2,1)S(1)} reshape(bf16[48,18,2048]{2,1,0:T(8,128)(2,1)} %convolution_convert_fusion) | data formatting | bytes 7077888 | tf_op jit(solution)/shard_map/convert_element_type | solution.py:43
  313.8 4.0 %fusion.14 = f32[2048,512]{1,0:T(8,128)S(1)} fusion(bf16[864,2048]{1,0:T(8,128)(2,1)S(1)} %convert_element_type.12, bf16[864,1,512]{2,1,0:T(2,128)(2,1)} %get-tuple-element.25), kind=kOutput, calls=%fused_computation.20 | convolution fusion | flops 1811939328 | bytes 8617984 | tf_op jit(solution)/shard_map/dot_general | solution.py:65
  317.8 2.4 fusion.15
  320.2 1.2 fusion.11
  321.5 0.2 pad_maximum_fusion
  321.7 2.2 copy.39
  323.9 54.2 %all_to_all.18 = bf16[1024,2,512]{2,1,0:T(2,128)(2,1)S(1)} all-to-all(bf16[1024,2,512]{2,1,0:T(2,128)(2,1)S(1)} %copy.39), channel_id=1, replica_groups=mesh['ga'=2,'band'=16] {'band'}, dimensions={0} | all-to-all | bytes 4194304 | tf_op jit(solution)/shard_map/all_to_all | solution.py:92
  378.0 3.6 copy.124
  (43 shorter events, 0.7 us)
Async XLA Ops:
  6.5 290.5 %all-reduce.2.cloned.1.call-start = ((), (), s32[]{:S(2)}) async-start(), calls=%async_computation.1 | async-start | bytes 18874368 | tf_op jit(solution)/shard_map/psum | solution.py:89
  16.1 11.7 %collective-permute-start = (bf16[64,2,512]{2,0,1:T(8,128)(2,1)S(1)}, bf16[64,2,512]{2,0,1:T(8,128)(2,1)S(1)}, u32[]{:S(2)}, u32[]{:S(2)}) collective-permute-start(bf16[64,2,512]{2,0,1:T(8,128)(2,1)S(1)} %bitcast.155), channel_id=1, source_target_pairs={{0,1},{1,0},{2,3},{3,2},{4,5},{5,4},{6,7},{7,6},{8,9},{9,8},{10,11... | collective-permute-start | bytes 393224 | tf_op jit(solution)/shard_map/ppermute | solution.py:81
  19.1 11.9 %collective-permute-start.1 = (bf16[64,2,512]{2,0,1:T(8,128)(2,1)S(1)}, bf16[64,2,512]{2,0,1:T(8,128)(2,1)S(1)}, u32[]{:S(2)}, u32[]{:S(2)}) collective-permute-start(bf16[64,2,512]{2,0,1:T(8,128)(2,1)S(1)} %bitcast.154), channel_id=1, source_target_pairs={{0,2},{1,3},{2,0},{3,1},{4,6},{5,7},{6,4},{7,5},{8,10},{9,11},{10,... | collective-permute-start | bytes 393224 | tf_op jit(solution)/shard_map/ppermute | solution.py:81
  20.8 10.9 %collective-permute-start.2 = (bf16[64,2,512]{2,0,1:T(8,128)(2,1)S(1)}, bf16[64,2,512]{2,0,1:T(8,128)(2,1)S(1)}, u32[]{:S(2)}, u32[]{:S(2)}) collective-permute-start(bf16[64,2,512]{2,0,1:T(8,128)(2,1)S(1)} %bitcast.153), channel_id=1, source_target_pairs={{0,3},{1,2},{2,1},{3,0},{4,7},{5,6},{6,5},{7,4},{8,11},{9,10},{10,... | collective-permute-start | bytes 393224 | tf_op jit(solution)/shard_map/ppermute | solution.py:81
  20.9 14.4 %collective-permute-start.3 = (bf16[64,2,512]{2,0,1:T(8,128)(2,1)S(1)}, bf16[64,2,512]{2,0,1:T(8,128)(2,1)S(1)}, u32[]{:S(2)}, u32[]{:S(2)}) collective-permute-start(bf16[64,2,512]{2,0,1:T(8,128)(2,1)S(1)} %bitcast.152), channel_id=1, source_target_pairs={{0,4},{1,5},{2,6},{3,7},{4,0},{5,1},{6,2},{7,3},{8,12},{9,13},{10,... | collective-permute-start | bytes 393224 | tf_op jit(solution)/shard_map/ppermute | solution.py:81
  23.0 14.2 %collective-permute-start.4 = (bf16[64,2,512]{2,0,1:T(8,128)(2,1)S(1)}, bf16[64,2,512]{2,0,1:T(8,128)(2,1)S(1)}, u32[]{:S(2)}, u32[]{:S(2)}) collective-permute-start(bf16[64,2,512]{2,0,1:T(8,128)(2,1)S(1)} %bitcast.151), channel_id=1, source_target_pairs={{0,5},{1,4},{2,7},{3,6},{4,1},{5,0},{6,3},{7,2},{8,13},{9,12},{10,... | collective-permute-start | bytes 393224 | tf_op jit(solution)/shard_map/ppermute | solution.py:81
  24.5 1.5 copy-start
  27.7 13.7 %collective-permute-start.5 = (bf16[64,2,512]{2,0,1:T(8,128)(2,1)S(1)}, bf16[64,2,512]{2,0,1:T(8,128)(2,1)S(1)}, u32[]{:S(2)}, u32[]{:S(2)}) collective-permute-start(bf16[64,2,512]{2,0,1:T(8,128)(2,1)S(1)} %bitcast.150), channel_id=1, source_target_pairs={{0,6},{1,7},{2,4},{3,5},{4,2},{5,3},{6,0},{7,1},{8,14},{9,15},{10,... | collective-permute-start | bytes 393224 | tf_op jit(solution)/shard_map/ppermute | solution.py:81
  31.0 11.1 %collective-permute-start.6 = (bf16[64,2,512]{2,0,1:T(8,128)(2,1)S(1)}, bf16[64,2,512]{2,0,1:T(8,128)(2,1)S(1)}, u32[]{:S(2)}, u32[]{:S(2)}) collective-permute-start(bf16[64,2,512]{2,0,1:T(8,128)(2,1)S(1)} %bitcast.149), channel_id=1, source_target_pairs={{0,7},{1,6},{2,5},{3,4},{4,3},{5,2},{6,1},{7,0},{8,15},{9,14},{10,... | collective-permute-start | bytes 393224 | tf_op jit(solution)/shard_map/ppermute | solution.py:81
  31.7 22.0 %collective-permute-start.7 = (bf16[64,2,512]{2,0,1:T(8,128)(2,1)S(1)}, bf16[64,2,512]{2,0,1:T(8,128)(2,1)S(1)}, u32[]{:S(2)}, u32[]{:S(2)}) collective-permute-start(bf16[64,2,512]{2,0,1:T(8,128)(2,1)S(1)} %bitcast.148), channel_id=1, source_target_pairs={{0,8},{1,9},{2,10},{3,11},{4,12},{5,13},{6,14},{7,15},{8,0},{9,1},... | collective-permute-start | bytes 393224 | tf_op jit(solution)/shard_map/ppermute | solution.py:81
  35.3 23.0 %collective-permute-start.8 = (bf16[64,2,512]{2,0,1:T(8,128)(2,1)S(1)}, bf16[64,2,512]{2,0,1:T(8,128)(2,1)S(1)}, u32[]{:S(2)}, u32[]{:S(2)}) collective-permute-start(bf16[64,2,512]{2,0,1:T(8,128)(2,1)S(1)} %bitcast.147), channel_id=1, source_target_pairs={{0,9},{1,8},{2,11},{3,10},{4,13},{5,12},{6,15},{7,14},{8,1},{9,0},... | collective-permute-start | bytes 393224 | tf_op jit(solution)/shard_map/ppermute | solution.py:81
  37.2 29.6 %collective-permute-start.9 = (bf16[64,2,512]{2,0,1:T(8,128)(2,1)S(1)}, bf16[64,2,512]{2,0,1:T(8,128)(2,1)S(1)}, u32[]{:S(2)}, u32[]{:S(2)}) collective-permute-start(bf16[64,2,512]{2,0,1:T(8,128)(2,1)S(1)} %bitcast.146), channel_id=1, source_target_pairs={{0,10},{1,11},{2,8},{3,9},{4,14},{5,15},{6,12},{7,13},{8,2},{9,3},... | collective-permute-start | bytes 393224 | tf_op jit(solution)/shard_map/ppermute | solution.py:81
  41.4 29.8 %collective-permute-start.10 = (bf16[64,2,512]{2,0,1:T(8,128)(2,1)S(1)}, bf16[64,2,512]{2,0,1:T(8,128)(2,1)S(1)}, u32[]{:S(2)}, u32[]{:S(2)}) collective-permute-start(bf16[64,2,512]{2,0,1:T(8,128)(2,1)S(1)} %bitcast.145), channel_id=1, source_target_pairs={{0,11},{1,10},{2,9},{3,8},{4,15},{5,14},{6,13},{7,12},{8,3},{9,2},... | collective-permute-start | bytes 393224 | tf_op jit(solution)/shard_map/ppermute | solution.py:81
  42.1 29.8 %collective-permute-start.11 = (bf16[64,2,512]{2,0,1:T(8,128)(2,1)S(1)}, bf16[64,2,512]{2,0,1:T(8,128)(2,1)S(1)}, u32[]{:S(2)}, u32[]{:S(2)}) collective-permute-start(bf16[64,2,512]{2,0,1:T(8,128)(2,1)S(1)} %bitcast.144), channel_id=1, source_target_pairs={{0,12},{1,13},{2,14},{3,15},{4,8},{5,9},{6,10},{7,11},{8,4},{9,5},... | collective-permute-start | bytes 393224 | tf_op jit(solution)/shard_map/ppermute | solution.py:81
  53.7 18.9 %collective-permute-start.12 = (bf16[64,2,512]{2,0,1:T(8,128)(2,1)S(1)}, bf16[64,2,512]{2,0,1:T(8,128)(2,1)S(1)}, u32[]{:S(2)}, u32[]{:S(2)}) collective-permute-start(bf16[64,2,512]{2,0,1:T(8,128)(2,1)S(1)} %bitcast.143), channel_id=1, source_target_pairs={{0,13},{1,12},{2,15},{3,14},{4,9},{5,8},{6,11},{7,10},{8,5},{9,4},... | collective-permute-start | bytes 393224 | tf_op jit(solution)/shard_map/ppermute | solution.py:81
  58.3 14.9 %collective-permute-start.13 = (bf16[64,2,512]{2,0,1:T(8,128)(2,1)S(1)}, bf16[64,2,512]{2,0,1:T(8,128)(2,1)S(1)}, u32[]{:S(2)}, u32[]{:S(2)}) collective-permute-start(bf16[64,2,512]{2,0,1:T(8,128)(2,1)S(1)} %bitcast.142), channel_id=1, source_target_pairs={{0,14},{1,15},{2,12},{3,13},{4,10},{5,11},{6,8},{7,9},{8,6},{9,7},... | collective-permute-start | bytes 393224 | tf_op jit(solution)/shard_map/ppermute | solution.py:81
  66.8 8.7 %collective-permute-start.14 = (bf16[64,2,512]{2,0,1:T(8,128)(2,1)S(1)}, bf16[64,2,512]{2,0,1:T(8,128)(2,1)S(1)}, u32[]{:S(2)}, u32[]{:S(2)}) collective-permute-start(bf16[64,2,512]{2,0,1:T(8,128)(2,1)S(1)} %bitcast.141), channel_id=1, source_target_pairs={{0,15},{1,14},{2,13},{3,12},{4,11},{5,10},{6,9},{7,8},{8,7},{9,6},... | collective-permute-start | bytes 393224 | tf_op jit(solution)/shard_map/ppermute | solution.py:81
  81.0 1.5 copy-start.3
  102.7 0.8 copy-start.4
  102.7 1.0 copy-start.5
  102.8 1.0 copy-start.6
  102.8 1.9 copy-start.1
  313.7 4.1 %copy-start.2 = (bf16[864,1,512]{2,1,0:T(2,128)(2,1)S(1)}, bf16[864,1,512]{2,1,0:T(2,128)(2,1)}, u32[]{:S(2)}) copy-start(bf16[864,1,512]{2,1,0:T(2,128)(2,1)} %get-tuple-element.26) | copy-start | bytes 2654212
Sparse Core Ops, SparseCore 0:
  102.9 194.1 all-reduce.1
